TPU v7x, 32 devices: a whole 2x2x4 slice. The times are simulated.
32 devices in a mesh: rows: 8 (over y, x, core), cols: 4 (over z).
Axes of the slice: x: 2, y: 2, z: 4, core: 2. Of those that a mesh axis runs over, the one named last changes fastest.
Arguments:
- token_ids: int32 [16, 2048], P('rows', 'cols'), may hold values from 0 to 131071, as said below
- lengths: int32 [16], P('rows'), may hold values from 1 to 2048
- table: bfloat16 [131072, 512], P('rows', 'cols'), may hold values from -6 to 6
- attn_gain: float32 [512], replicated, may hold values from 0.1 to 1.9
- w_qkv: bfloat16 [512, 1536], replicated, may hold values from -2 to 2
- w_out: bfloat16 [512, 512], replicated, may hold values from -0.25 to 0.25
- mlp_gain: float32 [512], replicated, may hold values from 0.1 to 1.9
- w_in: bfloat16 [512, 4096], replicated, may hold values from -0.25 to 0.25
- w_down: bfloat16 [2048, 512], replicated, may hold values from -0.125 to 0.125
Outputs:
- layer_out: bfloat16 [16, 2048, 512], P('rows', 'cols')
Inputs may be any that keep to these rules, and one draw needn't show every extreme that they name: `token_ids`: ids lie in 0 to 131071. In each aligned block of 2 histories (4096 positions) at most 1365 ids fall in any one block of 16384 consecutive table rows, and in every such block of histories some block of table rows receives exactly 1365.
All inputs are finite; a program needn't handle non-finite values.
Results may differ from a plain program's by a relative error of at most 0.012.
Values may be sent and summed in bfloat16 or wider, within the bound.
A program may use at most 192 MiB of HBM per device.

v0:
```python
import jax
import jax.numpy as jnp
from jax import lax
from jax.sharding import PartitionSpec as P

D = 512
HEADS = 8
FF = 2048


def rms_norm(values_f32, gain):
    mean_sq = jnp.mean(values_f32 * values_f32, axis=-1, keepdims=True)
    return values_f32 * lax.rsqrt(mean_sq + 1e-06) * gain


def local(token_ids, lengths, table, attn_gain, w_qkv, w_out, mlp_gain, w_in, w_down):
    batch_dev, quarter = token_ids.shape
    col_count = lax.axis_size("cols")
    row_count = lax.axis_size("rows")
    full_len = quarter * col_count
    block_rows, col_width = table.shape
    zero_bf = jnp.zeros((), jnp.bfloat16)
    own_ids = lax.all_gather(token_ids, "cols", axis=1, tiled=True)
    flat_ids = own_ids.reshape(-1)
    token_count = flat_ids.shape[0]
    capacity = 8 * token_count // (3 * row_count)
    owner_block = flat_ids // block_rows
    onehot = (owner_block[:, None] == jnp.arange(row_count, dtype=jnp.int32)[None, :]).astype(
        jnp.int32
    )
    slot_rank = jnp.sum((jnp.cumsum(onehot, axis=0) - 1) * onehot, axis=1)
    slot_index = owner_block * capacity + slot_rank
    requests = jnp.full((row_count * capacity,), -1, jnp.int32)
    requests = (
        requests.at[slot_index]
        .set(flat_ids - owner_block * block_rows)
        .reshape(row_count, capacity)
    )
    asked = lax.all_to_all(requests, "rows", split_axis=0, concat_axis=0, tiled=True)
    looked = jnp.take(table, jnp.maximum(asked, 0), axis=0)
    looked = jnp.where((asked >= 0)[..., None], looked, zero_bf)
    returned = lax.all_to_all(looked, "rows", split_axis=0, concat_axis=0, tiled=True)
    embedded = returned.reshape(row_count * capacity, col_width)[slot_index]
    embedded = embedded.reshape(batch_dev, full_len, col_width)
    sequence = lax.all_to_all(embedded, "cols", split_axis=1, concat_axis=2, tiled=True)
    residual = sequence.astype(jnp.float32)
    normed = rms_norm(residual, attn_gain).astype(jnp.bfloat16)
    projected = jnp.einsum("bqe,ef->bqf", normed, w_qkv, preferred_element_type=jnp.float32).astype(
        jnp.bfloat16
    )
    head_dim = D // HEADS
    queries = projected[..., :D].reshape(batch_dev, quarter, HEADS, head_dim)
    keys = projected[..., D : 2 * D]
    values = projected[..., 2 * D :]
    query_pos = lax.axis_index("cols") * quarter + jnp.arange(quarter, dtype=jnp.int32)
    running_max = jnp.full((batch_dev, HEADS, quarter), -1e30, jnp.float32)
    key_piece = lax.all_gather(keys, "cols", axis=1, tiled=True)
    value_piece = lax.all_gather(values, "cols", axis=1, tiled=True)
    piece_len = key_piece.shape[1]
    key_heads = key_piece.reshape(batch_dev, piece_len, HEADS, head_dim)
    value_heads = value_piece.reshape(batch_dev, piece_len, HEADS, head_dim)
    scores = (
        jnp.einsum("bqhd,bkhd->bhqk", queries, key_heads, preferred_element_type=jnp.float32)
        * 0.125
    )
    key_pos = jnp.arange(piece_len, dtype=jnp.int32)
    causal = key_pos[None, :] <= query_pos[:, None]
    inside = key_pos[None, :] < lengths[:, None]
    valid = causal[None, None, :, :] & inside[:, None, None, :]
    scores = jnp.where(valid, scores, -1e30)
    new_max = jnp.maximum(running_max, jnp.max(scores, axis=-1))
    probs = jnp.where(valid, jnp.exp(scores - new_max[..., None]), 0.0)
    running_sum = jnp.sum(probs, axis=-1)
    weighted = jnp.einsum(
        "bhqk,bkhd->bhqd",
        probs.astype(jnp.bfloat16),
        value_heads,
        preferred_element_type=jnp.float32,
    )
    final_max, final_sum, weighted = (new_max, running_sum, weighted)
    summed = weighted / final_sum[..., None]
    attended = (
        jnp.transpose(summed, (0, 2, 1, 3)).reshape(batch_dev, quarter, D).astype(jnp.bfloat16)
    )
    hidden = (
        residual + jnp.einsum("bqe,ef->bqf", attended, w_out, preferred_element_type=jnp.float32)
    ).astype(jnp.bfloat16)
    hidden_f32 = hidden.astype(jnp.float32)
    normed_two = rms_norm(hidden_f32, mlp_gain).astype(jnp.bfloat16)
    gate_up = jnp.einsum("bqe,ef->bqf", normed_two, w_in, preferred_element_type=jnp.float32)
    act = (jax.nn.silu(gate_up[..., :FF]) * gate_up[..., FF:]).astype(jnp.bfloat16)
    return (
        hidden_f32 + jnp.einsum("bqf,fe->bqe", act, w_down, preferred_element_type=jnp.float32)
    ).astype(jnp.bfloat16)


def solution(mesh):
    in_specs = (P("rows", "cols"), P("rows"), P("rows", "cols"), P(), P(), P(), P(), P(), P())
    out_specs = P("rows", "cols", None)
    return jax.shard_map(local, mesh=mesh, in_specs=in_specs, out_specs=out_specs, check_vma=False)
```

profile of v0, /device:TPU:0, one launch (start us, length us, event | category | flops | bytes accessed | tf_op | source)
XLA Modules:
  0.0 414.5 jit_solution(13161058633130101524)
XLA Ops:
  6.5 15.2 %all_gather.9 = s32[2,2048]{1,0:T(2,128)S(1)} all-gather(s32[2,512]{1,0:T(2,128)} %param.9), channel_id=1, replica_groups=mesh['rows'=8,'cols'=4] {'cols'}, dimensions={1}, use_global_device_ids=true | all-gather | bytes 20480 | tf_op jit(solution)/shard_map/all_gather | solution.py:23
  21.8 2.3 reduce-window.6
  24.1 0.3 slice_reduce_fusion
  24.4 0.2 reduce-window.9
  24.6 0.1 add_bitcast_fusion
  24.8 0.1 fusion.32
  24.9 0.1 compare_select_fusion
  25.0 15.5 %scatter_custom_fusion = s32[10920]{0:T(1024)S(1)} fusion(s32[4096]{0:T(1024)S(1)} %bitcast.81, s32[4096]{0:T(1024)S(1)} %get-tuple-element.10, s32[]{:T(128)} %constant.27.clone.1), kind=kCustom, calls=%fused_computation.65 | custom fusion | bytes 43684 | tf_op jit(solution)/shard_map/scatter | solution.py:36
  40.5 0.1 all_to_all.16
  40.6 8.4 %all_to_all.23 = s32[8,1,1365]{2,1,0:T(1,128)S(1)} all-to-all(s32[8,1,1365]{2,1,0:T(1,128)S(1)} %all_to_all.16), channel_id=1, replica_groups=mesh['rows'=8,'cols'=4] {'rows'}, dimensions={0} | all-to-all | bytes 87360 | tf_op jit(solution)/shard_map/all_to_all | solution.py:39
  49.1 0.1 reshape.265
  49.2 23.7 %gather_fusion = bf16[10920,128]{1,0:T(8,128)(2,1)} fusion(bf16[16384,128]{1,0:T(8,128)(2,1)} %param.11, s32[11264]{0:T(1024)S(1)} %pad_clamp_fusion), kind=kCustom, calls=%fused_computation | custom fusion | bytes 5634720 | tf_op jit(solution)/shard_map/jit(_take)/gather | solution.py:40
  72.9 4.2 %reshape.264 = bf16[8,1365,128]{2,1,0:T(8,128)(2,1)} reshape(bf16[10920,128]{1,0:T(8,128)(2,1)} %gather_fusion) | data formatting | bytes 5591040 | tf_op jit(solution)/shard_map/jit(_take)/gather | solution.py:40
  77.1 10.2 %select_select_fusion = bf16[8,1365,128]{2,1,0:T(8,128)(2,1)} fusion(bf16[8,1365,128]{2,1,0:T(8,128)(2,1)} %reshape.264, pred[8,1365]{1,0:T(8,128)(4,1)S(1)} %get-tuple-element.9, pred[8,1365]{1,0:T(8,128)(4,1)S(1)} %get-tuple-element.8), kind=kLoop, calls=%fused_computation.21 | loop fusion | flops 2795520 | bytes 5612880 | tf_op jit(solution)/shard_map/jit(_where)/select_n | solution.py:41
  87.3 4.4 %all-to-all-start.1 = ((bf16[8,1365,128]{2,1,0:T(8,128)(2,1)}), bf16[8,1365,128]{2,1,0:T(8,128)(2,1)}, u32[]{:S(2)}, u32[]{:S(2)}) async-start(bf16[8,1365,128]{2,1,0:T(8,128)(2,1)} %select_select_fusion), calls=%async_computation.1 | async-start | bytes 5603328 | tf_op jit(solution)/shard_map/all_to_all | solution.py:42
  91.7 0.0 all-gather.3.cloned.1.call-start
  91.8 34.1 %all-to-all-done.1 = bf16[8,1365,128]{2,1,0:T(8,128)(2,1)} async-done(((bf16[8,1365,128]{2,1,0:T(8,128)(2,1)}), bf16[8,1365,128]{2,1,0:T(8,128)(2,1)}, u32[]{:S(2)}, u32[]{:S(2)}) %all-to-all-start.1) | async-done | bytes 2795552 | tf_op jit(solution)/shard_map/all_to_all | solution.py:42
  125.9 4.2 %reshape.256 = bf16[10920,128]{1,0:T(8,128)(2,1)} reshape(bf16[8,1365,128]{2,1,0:T(8,128)(2,1)} %all-to-all-done.1) | data formatting | bytes 5591040 | tf_op jit(solution)/shard_map/reshape | solution.py:43
  130.1 13.2 %gather_fusion.1 = bf16[4096,128]{1,0:T(8,128)(2,1)S(1)} fusion(bf16[10920,128]{1,0:T(8,128)(2,1)} %reshape.256, s32[4096]{0:T(1024)S(1)} %broadcast_clamp_fusion), kind=kCustom, calls=%fused_computation.1 | custom fusion | bytes 2113536 | tf_op jit(solution)/shard_map/gather | solution.py:43
  143.3 8.7 %copy.57 = bf16[2,2048,128]{2,0,1:T(2,128)(2,1)S(1)} copy(bf16[2,2048,128]{2,1,0:T(8,128)(2,1)S(1)} %bitcast.75) | data formatting | bytes 2097152 | tf_op jit(solution)/shard_map/reshape | solution.py:44
  152.0 27.2 %all_to_all.24 = bf16[2,2048,128]{2,0,1:T(2,128)(2,1)S(1)} all-to-all(bf16[2,2048,128]{2,0,1:T(2,128)(2,1)S(1)} %copy.57), channel_id=1, replica_groups=mesh['rows'=8,'cols'=4] {'cols'}, dimensions={1} | all-to-all | bytes 2097152 | tf_op jit(solution)/shard_map/all_to_all | solution.py:45
  179.2 1.5 copy_convert_fusion
  180.7 2.9 copy.59
  183.6 0.6 multiply_reduce_fusion
  184.3 1.8 fusion.18
  186.2 3.2 convolution_convert_fusion
  189.4 0.0 copy-start.3
  189.4 1.7 fusion.44
  191.1 0.0 all-gather.3.cloned.1.call-update
  191.1 0.0 all-gather.5.cloned.1.call-start
  191.2 0.1 iota_compare_fusion.3
  191.3 0.7 iota_compare_fusion
  191.9 2.6 broadcast_and_fusion
  194.6 1.3 copy.61
  195.9 0.0 all-gather.5.cloned.1.call-update
  195.9 76.4 %all-gather.3.cloned.1.call-done = bf16[2,2048,512]{2,1,0:T(8,128)(2,1)} async-done(((bf16[2,512,512]{2,1,0:T(8,128)(2,1)}), bf16[2,2048,512]{2,1,0:T(8,128)(2,1)}) %all-gather.3.cloned.1.call-update) | async-done | bytes 4194320 | tf_op jit(solution)/shard_map/all_gather | solution.py:57
  272.4 6.3 %copy.62 = bf16[2,2048,512]{1,2,0:T(8,128)(2,1)} copy(bf16[2,2048,512]{2,1,0:T(8,128)(2,1)} %all-gather.3.cloned.1.call-done) | data formatting | bytes 8388608 | tf_op jit(solution)/shard_map/all_gather | solution.py:57
  278.6 27.7 %fusion = (f32[2,8,512]{2,1,0:T(8,128)S(1)}, f32[2,8,512,2048]{3,2,1,0:T(8,128)}) fusion(pred[2,512,2048]{2,1,0:T(8,128)(4,1)} %broadcast_and_fusion, bf16[2,512,8,64]{1,3,2,0:T(8,128)(2,1)} %bitcast.74, bf16[2,2048,8,64]{1,3,2,0:T(8,128)(2,1)} %bitcast.72), kind=kOutput, calls=%fused_computation.5 | convolution fusion | flops 2197807104 | bytes 74481664 | tf_op jit(solution)/shard_map/bqhd,bkhd->bhqk/dot_general | solution.py:63
  306.3 22.4 %fusion.1 = f32[2,8,512]{2,1,0:T(8,128)S(1)} fusion(f32[2,8,512,2048]{3,2,1,0:T(8,128)} %get-tuple-element.13, f32[2,8,512]{2,1,0:T(8,128)S(1)} %broadcast_maximum_fusion, pred[2,512,2048]{2,1,0:T(8,128)(4,1)S(1)} %copy-done.1), kind=kLoop, calls=%fused_computation.6 | loop fusion | flops 83877888 | bytes 69271552 | tf_op jit(solution)/shard_map/reduce_sum | solution.py:73
  328.7 24.5 %all-gather.5.cloned.1.call-done = bf16[2,2048,512]{2,1,0:T(8,128)(2,1)} async-done(((bf16[2,512,512]{2,1,0:T(8,128)(2,1)}), bf16[2,2048,512]{2,1,0:T(8,128)(2,1)}) %all-gather.5.cloned.1.call-update) | async-done | bytes 4194320 | tf_op jit(solution)/shard_map/all_gather | solution.py:58
  353.2 6.3 %copy.63 = bf16[2,2048,512]{1,2,0:T(8,128)(2,1)} copy(bf16[2,2048,512]{2,1,0:T(8,128)(2,1)} %all-gather.5.cloned.1.call-done) | data formatting | bytes 8388608 | tf_op jit(solution)/shard_map/all_gather | solution.py:58
  359.5 27.0 %fusion.16 = bf16[2,512,8,64]{1,3,2,0:T(8,128)(2,1)S(1)} fusion(bf16[2,2048,8,64]{1,3,2,0:T(8,128)(2,1)} %bitcast.76, f32[2,8,512,2048]{3,2,1,0:T(8,128)} %get-tuple-element.13, f32[2,8,512]{2,1,0:T(8,128)S(1)} %broadcast_maximum_fusion, pred[2,512,2048]{2,1,0:T(8,128)(4,1)} %broadcast_and_fusion, f32[2,512,8]{1,2,0:T(8,128)S(1)} %bitcast.85), kind=kOutput, calls=%fused_computation.28 | convolution fusion | flops 2232418304 | bytes 74514432 | tf_op jit(solution)/shard_map/bhqk,bkhd->bhqd/dot_general | solution.py:74
  386.5 0.0 copy-start.5
  386.5 2.7 fusion.11
  389.2 0.3 copy-done.4
  389.4 8.3 %fusion.7 = f32[2,512,4096]{2,1,0:T(8,128)} fusion(bf16[512,4096]{1,0:T(8,128)(2,1)S(1)} %copy-done.4, bf16[2,512,512]{1,2,0:T(8,128)(2,1)S(1)} %get-tuple-element.15, f32[512]{0:T(512)S(1)} %copy-done.5, f32[2,512]{1,0:T(2,128)S(1)} %add_rsqrt_fusion), kind=kOutput, calls=%fused_computation.12 | convolution fusion | flops 4297064448 | bytes 22026240 | tf_op jit(solution)/shard_map/bqe,ef->bqf/dot_general | solution.py:90
  397.8 8.6 %fusion.14 = bf16[2,512,512]{1,2,0:T(8,128)(2,1)S(1)} fusion(bf16[2,512,512]{1,2,0:T(8,128)(2,1)S(1)} %get-tuple-element.15, bf16[2048,512]{1,0:T(8,128)(2,1)S(1)} %copy-done, f32[2,512,4096]{2,1,0:T(8,128)} %fusion.7), kind=kOutput, calls=%fused_computation.25 | convolution fusion | flops 2161639424 | bytes 20971520 | tf_op jit(solution)/shard_map/bqf,fe->bqe/dot_general | solution.py:93
  406.3 1.3 copy.68
  (25 shorter events, 0.2 us)
Async XLA Ops:
  6.5 391.2 %copy-start = (bf16[2048,512]{1,0:T(8,128)(2,1)S(1)}, bf16[2048,512]{1,0:T(8,128)(2,1)}, u32[]{:S(2)}) copy-start(bf16[2048,512]{1,0:T(8,128)(2,1)} %param.17) | copy-start | bytes 6291460
  87.3 38.6 %all-to-all-start.1 = ((bf16[8,1365,128]{2,1,0:T(8,128)(2,1)}), bf16[8,1365,128]{2,1,0:T(8,128)(2,1)}, u32[]{:S(2)}, u32[]{:S(2)}) async-start(bf16[8,1365,128]{2,1,0:T(8,128)(2,1)} %select_select_fusion), calls=%async_computation.1 | async-start | bytes 5603328 | tf_op jit(solution)/shard_map/all_to_all | solution.py:42
  91.7 180.7 %all-gather.3.cloned.1.call-start = ((), (), s32[]{:S(2)}) async-start(), calls=%async_computation.3 | async-start | bytes 5242880 | tf_op jit(solution)/shard_map/all_gather | solution.py:57
  179.2 5.1 %copy-start.2 = (f32[512]{0:T(512)S(1)}, f32[512]{0:T(512)}, u32[]{:S(2)}) copy-start(f32[512]{0:T(512)} %param.12) | copy-start | bytes 6148
  189.4 1.8 copy-start.3
  191.1 162.1 %all-gather.5.cloned.1.call-start = ((), (), s32[]{:S(2)}) async-start(), calls=%async_computation.4 | async-start | bytes 5242880 | tf_op jit(solution)/shard_map/all_gather | solution.py:58
  278.6 27.7 %copy-start.1 = (pred[2,512,2048]{2,1,0:T(8,128)(4,1)S(1)}, pred[2,512,2048]{2,1,0:T(8,128)(4,1)}, u32[]{:S(2)}) copy-start(pred[2,512,2048]{2,1,0:T(8,128)(4,1)} %broadcast_and_fusion) | copy-start | bytes 6291460
  386.5 3.0 copy-start.4
  386.5 3.0 copy-start.5
Sparse Core Ops, SparseCore 0:
  191.2 81.0 all-gather.2
  273.9 79.2 all-gather.4
where the time goes:
time: 415 us
  waiting for transfers between devices  135 us (33%)
  local copies, waits for them, and re-layouts  90.2 us (22%)
  matrix products  77.4 us (19%)
  blocking collectives  50.8 us (12%)
  other arithmetic  42.8 us (10%)
  between operations  13.7 us (3%)
  starting transfers between devices  4.49 us (1%)
    all_gather x1, waiting for transfers between devices, local(): key_piece = lax.all_gather(keys, 'cols', axis=1, tiled=True)  76.4 us
    all_to_all x1, waiting for transfers between devices, local(): lax.all_to_all(looked, 'rows', split_axis=0, concat_axis=0, tiled=True)  34.1 us
    gather x2, local copies, waits for them, and re-layouts, local(): looked = jnp.take(table, jnp.maximum(asked, 0), axis=0)  27.9 us
    dot_general x1, matrix products, local(): jnp.einsum('bqhd,bkhd->bhqk', queries, key_heads, preferred_element_type=...  27.7 us
    all_to_all x1, blocking collectives, local(): lax.all_to_all(embedded, 'cols', split_axis=1, concat_axis=2, tiled=True)  27.2 us
    dot_general x1, matrix products, local(): jnp.einsum('bhqk,bkhd->bhqd', probs.astype(jnp.bfloat16), value_heads, pr...  27 us
    all_gather x1, waiting for transfers between devices, local(): value_piece = lax.all_gather(values, 'cols', axis=1, tiled=True)  24.5 us
    reduce_sum x1, other arithmetic, local(): running_sum = jnp.sum(probs, axis=-1)  22.4 us
  transfers between devices with their start and end apart: 3, of which 3 were waited for; matrix products, arithmetic and copies ran while one was open for 15% of the time, Pallas kernels for 0%

commit v1 on v0

--- a/solution.py
+++ b/solution.py
@@ -6,6 +6,18 @@
 D = 512
 HEADS = 8
 FF = 2048
+
+
+def cut_along(shard, dim, size):
+    dims = shard.shape
+    parts = shard.reshape(*dims[:dim], size, dims[dim] // size, *dims[dim + 1 :])
+    return jnp.moveaxis(parts, dim, 0)
+
+
+def in_order(blocks, dim):
+    shape = list(blocks.shape[1:])
+    shape[dim] *= blocks.shape[0]
+    return jnp.moveaxis(blocks, 0, dim).reshape(shape)
 
 
 def rms_norm(values_f32, gain):
@@ -42,7 +54,14 @@
     returned = lax.all_to_all(looked, "rows", split_axis=0, concat_axis=0, tiled=True)
     embedded = returned.reshape(row_count * capacity, col_width)[slot_index]
     embedded = embedded.reshape(batch_dev, full_len, col_width)
-    sequence = lax.all_to_all(embedded, "cols", split_axis=1, concat_axis=2, tiled=True)
+    size, index = (lax.axis_size("cols"), lax.axis_index("cols"))
+    blocks = cut_along(embedded, 1, size)
+    done = [blocks[index]]
+    for step in range(1, size):
+        sent = blocks[(index + step) % size]
+        done.append(lax.ppermute(sent, "cols", [(i, (i + step) % size) for i in range(size)]))
+    blocks = jnp.stack(done)[(index - jnp.arange(size)) % size]
+    sequence = in_order(blocks, 2)
     residual = sequence.astype(jnp.float32)
     normed = rms_norm(residual, attn_gain).astype(jnp.bfloat16)
     projected = jnp.einsum("bqe,ef->bqf", normed, w_qkv, preferred_element_type=jnp.float32).astype(

time: 415 us -> 404 us (0.973)
  blocking collectives: 50.8 us -> 23.6 us
  waiting for transfers between devices: 135 us -> 153 us
  local copies, waits for them, and re-layouts: 90.2 us -> 83.6 us
    all_to_all x1 -> x0, blocking collectives: 27.2 us -> none  [local(): lax.all_to_all(embedded, 'cols', split_axis=1, concat_axis=2, tiled=True)]
    ppermute x0 -> x3, waiting for transfers between devices: none -> 14.5 us  [local(): lax.ppermute(sent, 'cols', [(i, (i + step) % size) for i in range(size)])]
    reshape x1 -> x0, local copies, waits for them, and re-layouts: 8.68 us -> none  [local(): embedded = embedded.reshape(batch_dev, full_len, col_width)]
  transfers between devices with their start and end apart: 3 -> 6, of which waited for: 3 -> 4; matrix products, arithmetic and copies ran while one was open for 15% -> 15% of each run, Pallas kernels for 0% -> 0%
where the time goes in v1:
time: 404 us; the launch traced here: 403 us
  waiting for transfers between devices  153 us (38%)
  local copies, waits for them, and re-layouts  83.6 us (21%)
  matrix products  77.4 us (19%)
  other arithmetic  43.6 us (11%)
  blocking collectives  23.6 us (6%)
  between operations  13.7 us (3%)
  starting transfers between devices  8.5 us (2%)
    all_gather x1, waiting for transfers between devices, local(): key_piece = lax.all_gather(keys, 'cols', axis=1, tiled=True)  79.9 us
    all_to_all x1, waiting for transfers between devices, local(): lax.all_to_all(looked, 'rows', split_axis=0, concat_axis=0, tiled=True)  34.1 us
    gather x2, local copies, waits for them, and re-layouts, local(): looked = jnp.take(table, jnp.maximum(asked, 0), axis=0)  27.9 us
    dot_general x1, matrix products, local(): jnp.einsum('bqhd,bkhd->bhqk', queries, key_heads, preferred_element_type=...  27.7 us
    dot_general x1, matrix products, local(): jnp.einsum('bhqk,bkhd->bhqd', probs.astype(jnp.bfloat16), value_heads, pr...  27 us
    all_gather x1, waiting for transfers between devices, local(): value_piece = lax.all_gather(values, 'cols', axis=1, tiled=True)  24.5 us
    reduce_sum x1, other arithmetic, local(): running_sum = jnp.sum(probs, axis=-1)  22.4 us
    scatter x1, local copies, waits for them, and re-layouts, local(): requests = requests.at[slot_index].set(flat_ids - owner_block * block_row...  15.5 us
  transfers between devices with their start and end apart: 6, of which 4 were waited for; matrix products, arithmetic and copies ran while one was open for 15% of the time, Pallas kernels for 0%

profile of v1, /device:TPU:0, one launch (start us, length us, event | category | flops | bytes accessed | tf_op | source)
XLA Modules:
  0.0 403.5 jit_solution(5449553656300063628)
XLA Ops:
  6.5 15.2 %all_gather.9 = s32[2,2048]{1,0:T(2,128)S(1)} all-gather(s32[2,512]{1,0:T(2,128)} %param.9), channel_id=1, replica_groups=mesh['rows'=8,'cols'=4] {'cols'}, dimensions={1}, use_global_device_ids=true | all-gather | bytes 20480 | tf_op jit(solution)/shard_map/all_gather | solution.py:35
  21.8 2.3 reduce-window.6
  24.1 0.3 slice_reduce_fusion
  24.4 0.2 reduce-window.9
  24.6 0.1 add_bitcast_fusion
  24.8 0.1 fusion.33
  24.9 0.1 compare_select_fusion
  25.0 15.5 %scatter_custom_fusion = s32[10920]{0:T(1024)S(1)} fusion(s32[4096]{0:T(1024)S(1)} %bitcast.95, s32[4096]{0:T(1024)S(1)} %get-tuple-element.14, s32[]{:T(128)} %constant.85.clone.1), kind=kCustom, calls=%fused_computation.72 | custom fusion | bytes 43684 | tf_op jit(solution)/shard_map/scatter | solution.py:48
  40.5 0.1 all_to_all.9
  40.6 8.4 %all_to_all.14 = s32[8,1,1365]{2,1,0:T(1,128)S(1)} all-to-all(s32[8,1,1365]{2,1,0:T(1,128)S(1)} %all_to_all.9), channel_id=1, replica_groups=mesh['rows'=8,'cols'=4] {'rows'}, dimensions={0} | all-to-all | bytes 87360 | tf_op jit(solution)/shard_map/all_to_all | solution.py:51
  49.1 0.1 reshape.312
  49.2 23.7 %gather_fusion = bf16[10920,128]{1,0:T(8,128)(2,1)} fusion(bf16[16384,128]{1,0:T(8,128)(2,1)} %param.11, s32[11264]{0:T(1024)S(1)} %pad_clamp_fusion), kind=kCustom, calls=%fused_computation | custom fusion | bytes 5634720 | tf_op jit(solution)/shard_map/jit(_take)/gather | solution.py:52
  72.9 4.2 %reshape.311 = bf16[8,1365,128]{2,1,0:T(8,128)(2,1)} reshape(bf16[10920,128]{1,0:T(8,128)(2,1)} %gather_fusion) | data formatting | bytes 5591040 | tf_op jit(solution)/shard_map/jit(_take)/gather | solution.py:52
  77.1 10.2 %select_select_fusion = bf16[8,1365,128]{2,1,0:T(8,128)(2,1)} fusion(bf16[8,1365,128]{2,1,0:T(8,128)(2,1)} %reshape.311, pred[8,1365]{1,0:T(8,128)(4,1)S(1)} %get-tuple-element.13, pred[8,1365]{1,0:T(8,128)(4,1)S(1)} %get-tuple-element.12), kind=kLoop, calls=%fused_computation.22 | loop fusion | flops 2795520 | bytes 5612880 | tf_op jit(solution)/shard_map/jit(_where)/select_n | solution.py:53
  87.3 4.4 %all-to-all-start.1 = ((bf16[8,1365,128]{2,1,0:T(8,128)(2,1)}), bf16[8,1365,128]{2,1,0:T(8,128)(2,1)}, u32[]{:S(2)}, u32[]{:S(2)}) async-start(bf16[8,1365,128]{2,1,0:T(8,128)(2,1)} %select_select_fusion), calls=%async_computation.1 | async-start | bytes 5603328 | tf_op jit(solution)/shard_map/all_to_all | solution.py:54
  91.7 0.0 all-gather.3.cloned.1.call-start
  91.8 34.1 %all-to-all-done.1 = bf16[8,1365,128]{2,1,0:T(8,128)(2,1)} async-done(((bf16[8,1365,128]{2,1,0:T(8,128)(2,1)}), bf16[8,1365,128]{2,1,0:T(8,128)(2,1)}, u32[]{:S(2)}, u32[]{:S(2)}) %all-to-all-start.1) | async-done | bytes 2795552 | tf_op jit(solution)/shard_map/all_to_all | solution.py:54
  125.9 4.2 %reshape.305 = bf16[10920,128]{1,0:T(8,128)(2,1)} reshape(bf16[8,1365,128]{2,1,0:T(8,128)(2,1)} %all-to-all-done.1) | data formatting | bytes 5591040 | tf_op jit(solution)/shard_map/reshape | solution.py:55
  130.1 13.2 %gather_fusion.1 = bf16[4096,128]{1,0:T(8,128)(2,1)S(1)} fusion(bf16[10920,128]{1,0:T(8,128)(2,1)} %reshape.305, s32[4096]{0:T(1024)S(1)} %broadcast_clamp_fusion), kind=kCustom, calls=%fused_computation.1 | custom fusion | bytes 2113536 | tf_op jit(solution)/shard_map/gather | solution.py:55
  143.3 0.1 dynamic-slice_bitcast_fusion.3
  143.4 0.6 collective-permute-start.1
  144.0 3.4 collective-permute-start.2
  147.4 14.5 %collective-permute-done.1 = bf16[2,512,128]{2,1,0:T(8,128)(2,1)S(1)} collective-permute-done((bf16[2,512,128]{2,1,0:T(8,128)(2,1)S(1)}, bf16[2,512,128]{2,1,0:T(8,128)(2,1)S(1)}, u32[]{:S(2)}, u32[]{:S(2)}) %collective-permute-start.1) | collective-permute-done | bytes 262176 | tf_op jit(solution)/shard_map/ppermute | solution.py:62
  162.0 1.1 pad_maximum_fusion
  163.1 2.0 gather_fusion.2
  165.1 1.5 convert_bitcast_fusion
  166.6 0.3 fusion.11
  166.8 2.9 copy.41
  169.8 1.8 fusion.19
  171.6 3.2 convolution_convert_fusion
  174.9 1.7 fusion.47
  176.6 0.0 all-gather.5.cloned.1.call-start
  176.7 0.1 iota_compare_fusion.3
  176.7 0.7 iota_compare_fusion
  177.4 2.6 broadcast_and_fusion
  180.0 1.3 copy.43
  181.4 79.9 %all-gather.3.cloned.1.call-done = bf16[2,2048,512]{2,1,0:T(8,128)(2,1)} async-done(((bf16[2,512,512]{2,1,0:T(8,128)(2,1)}), bf16[2,2048,512]{2,1,0:T(8,128)(2,1)}) %all-gather.3.cloned.1.call-update) | async-done | bytes 4194320 | tf_op jit(solution)/shard_map/all_gather | solution.py:76
  261.3 6.3 %copy.44 = bf16[2,2048,512]{1,2,0:T(8,128)(2,1)} copy(bf16[2,2048,512]{2,1,0:T(8,128)(2,1)} %all-gather.3.cloned.1.call-done) | data formatting | bytes 8388608 | tf_op jit(solution)/shard_map/all_gather | solution.py:76
  267.6 27.7 %fusion = (f32[2,8,512]{2,1,0:T(8,128)S(1)}, f32[2,8,512,2048]{3,2,1,0:T(8,128)}) fusion(pred[2,512,2048]{2,1,0:T(8,128)(4,1)} %broadcast_and_fusion, bf16[2,512,8,64]{1,3,2,0:T(8,128)(2,1)} %bitcast.85, bf16[2,2048,8,64]{1,3,2,0:T(8,128)(2,1)} %bitcast.84), kind=kOutput, calls=%fused_computation.6 | convolution fusion | flops 2197807104 | bytes 74481664 | tf_op jit(solution)/shard_map/bqhd,bkhd->bhqk/dot_general | solution.py:82
  295.3 22.4 %fusion.1 = f32[2,8,512]{2,1,0:T(8,128)S(1)} fusion(f32[2,8,512,2048]{3,2,1,0:T(8,128)} %get-tuple-element.17, f32[2,8,512]{2,1,0:T(8,128)S(1)} %broadcast_maximum_fusion, pred[2,512,2048]{2,1,0:T(8,128)(4,1)S(1)} %copy-done.1), kind=kLoop, calls=%fused_computation.7 | loop fusion | flops 83877888 | bytes 69271552 | tf_op jit(solution)/shard_map/reduce_sum | solution.py:92
  317.6 24.5 %all-gather.5.cloned.1.call-done = bf16[2,2048,512]{2,1,0:T(8,128)(2,1)} async-done(((bf16[2,512,512]{2,1,0:T(8,128)(2,1)}), bf16[2,2048,512]{2,1,0:T(8,128)(2,1)}) %all-gather.5.cloned.1.call-update) | async-done | bytes 4194320 | tf_op jit(solution)/shard_map/all_gather | solution.py:77
  342.1 6.3 %copy.45 = bf16[2,2048,512]{1,2,0:T(8,128)(2,1)} copy(bf16[2,2048,512]{2,1,0:T(8,128)(2,1)} %all-gather.5.cloned.1.call-done) | data formatting | bytes 8388608 | tf_op jit(solution)/shard_map/all_gather | solution.py:77
  348.4 27.0 %fusion.17 = bf16[2,512,8,64]{1,3,2,0:T(8,128)(2,1)S(1)} fusion(bf16[2,2048,8,64]{1,3,2,0:T(8,128)(2,1)} %bitcast.87, f32[2,8,512,2048]{3,2,1,0:T(8,128)} %get-tuple-element.17, f32[2,8,512]{2,1,0:T(8,128)S(1)} %broadcast_maximum_fusion, pred[2,512,2048]{2,1,0:T(8,128)(4,1)} %broadcast_and_fusion, f32[2,512,8]{1,2,0:T(8,128)S(1)} %bitcast.99), kind=kOutput, calls=%fused_computation.32 | convolution fusion | flops 2232418304 | bytes 74514432 | tf_op jit(solution)/shard_map/bhqk,bkhd->bhqd/dot_general | solution.py:93
  375.4 2.7 fusion.12
  378.1 0.3 copy-done.4
  378.4 8.3 %fusion.7 = f32[2,512,4096]{2,1,0:T(8,128)} fusion(bf16[512,4096]{1,0:T(8,128)(2,1)S(1)} %copy-done.4, bf16[2,512,512]{1,2,0:T(8,128)(2,1)S(1)} %get-tuple-element.19, f32[512]{0:T(512)S(1)} %copy-done.5, f32[2,512]{1,0:T(2,128)S(1)} %add_rsqrt_fusion), kind=kOutput, calls=%fused_computation.13 | convolution fusion | flops 4297064448 | bytes 22026240 | tf_op jit(solution)/shard_map/bqe,ef->bqf/dot_general | solution.py:109
  386.7 8.6 %fusion.15 = bf16[2,512,512]{1,2,0:T(8,128)(2,1)S(1)} fusion(bf16[2,512,512]{1,2,0:T(8,128)(2,1)S(1)} %get-tuple-element.19, bf16[2048,512]{1,0:T(8,128)(2,1)S(1)} %copy-done, f32[2,512,4096]{2,1,0:T(8,128)} %fusion.7), kind=kOutput, calls=%fused_computation.29 | convolution fusion | flops 2161639424 | bytes 20971520 | tf_op jit(solution)/shard_map/bqf,fe->bqe/dot_general | solution.py:112
  395.3 1.3 copy.50
  (32 shorter events, 0.2 us)
Async XLA Ops:
  6.5 380.2 %copy-start = (bf16[2048,512]{1,0:T(8,128)(2,1)S(1)}, bf16[2048,512]{1,0:T(8,128)(2,1)}, u32[]{:S(2)}) copy-start(bf16[2048,512]{1,0:T(8,128)(2,1)} %param.17) | copy-start | bytes 6291460
  87.3 38.6 %all-to-all-start.1 = ((bf16[8,1365,128]{2,1,0:T(8,128)(2,1)}), bf16[8,1365,128]{2,1,0:T(8,128)(2,1)}, u32[]{:S(2)}, u32[]{:S(2)}) async-start(bf16[8,1365,128]{2,1,0:T(8,128)(2,1)} %select_select_fusion), calls=%async_computation.1 | async-start | bytes 5603328 | tf_op jit(solution)/shard_map/all_to_all | solution.py:54
  91.7 169.6 %all-gather.3.cloned.1.call-start = ((), (), s32[]{:S(2)}) async-start(), calls=%async_computation.2 | async-start | bytes 5242880 | tf_op jit(solution)/shard_map/all_gather | solution.py:76
  143.4 18.6 %collective-permute-start.1 = (bf16[2,512,128]{2,1,0:T(8,128)(2,1)S(1)}, bf16[2,512,128]{2,1,0:T(8,128)(2,1)S(1)}, u32[]{:S(2)}, u32[]{:S(2)}) collective-permute-start(bf16[2,512,128]{2,1,0:T(8,128)(2,1)S(1)} %get-tuple-element.10), channel_id=1, source_target_pairs={{0,2},{1,3},{2,0},{3,1},{4,6},{5,7},{6,4},{7,5},{8,10},{9,11},{10,... | collective-permute-start | bytes 786440 | tf_op jit(solution)/shard_map/ppermute | solution.py:62
  144.0 17.9 %collective-permute-start.2 = (bf16[2,512,128]{2,1,0:T(8,128)(2,1)S(1)}, bf16[2,512,128]{2,1,0:T(8,128)(2,1)S(1)}, u32[]{:S(2)}, u32[]{:S(2)}) collective-permute-start(bf16[2,512,128]{2,1,0:T(8,128)(2,1)S(1)} %get-tuple-element.9), channel_id=1, source_target_pairs={{0,3},{1,0},{2,1},{3,2},{4,7},{5,4},{6,5},{7,6},{8,11},{9,8},{10,9... | collective-permute-start | bytes 786440 | tf_op jit(solution)/shard_map/ppermute | solution.py:62
  147.4 14.6 %collective-permute-start = (bf16[2,512,128]{2,1,0:T(8,128)(2,1)S(1)}, bf16[2,512,128]{2,1,0:T(8,128)(2,1)S(1)}, u32[]{:S(2)}, u32[]{:S(2)}) collective-permute-start(bf16[2,512,128]{2,1,0:T(8,128)(2,1)S(1)} %get-tuple-element.11), channel_id=1, source_target_pairs={{0,1},{1,2},{2,3},{3,0},{4,5},{5,6},{6,7},{7,4},{8,9},{9,10},{10,1... | collective-permute-start | bytes 786440 | tf_op jit(solution)/shard_map/ppermute | solution.py:62
  165.1 4.7 %copy-start.2 = (f32[512]{0:T(512)S(1)}, f32[512]{0:T(512)}, u32[]{:S(2)}) copy-start(f32[512]{0:T(512)} %param.12) | copy-start | bytes 6148
  174.9 1.8 copy-start.3
  176.6 165.6 %all-gather.5.cloned.1.call-start = ((), (), s32[]{:S(2)}) async-start(), calls=%async_computation.3 | async-start | bytes 5242880 | tf_op jit(solution)/shard_map/all_gather | solution.py:77
  267.6 27.7 %copy-start.1 = (pred[2,512,2048]{2,1,0:T(8,128)(4,1)S(1)}, pred[2,512,2048]{2,1,0:T(8,128)(4,1)}, u32[]{:S(2)}) copy-start(pred[2,512,2048]{2,1,0:T(8,128)(4,1)} %broadcast_and_fusion) | copy-start | bytes 6291460
  375.4 3.0 copy-start.4
  375.4 3.0 copy-start.5
Sparse Core Ops, SparseCore 0:
  176.7 84.5 all-gather.2
  262.9 79.2 all-gather.4
